TPU v7x, 32 devices: a whole 2x2x4 slice. The times are simulated.
32 devices in a mesh: groups: 2 (over y), seq: 8 (over z, x), tp: 2 (over core).
Axes of the slice: x: 2, y: 2, z: 4, core: 2. Of those that a mesh axis runs over, the one named last changes fastest.
Arguments:
- span_queries: bfloat16 [128, 64, 128], P(('groups', 'seq'), 'tp'), parts along dimension 0, may hold values from -180 to 180
- span_keys: bfloat16 [128, 4, 128], P(('groups', 'seq'), 'tp'), parts along dimension 0, may hold values from -9 to 9
- span_values: bfloat16 [128, 4, 128], P(('groups', 'seq'), 'tp'), parts along dimension 0, may hold values from -6.5 to 6.5
- prefix_keys: bfloat16 [1152, 4, 128], P(('groups', 'seq'), 'tp'), parts along dimension 0, may hold values from -9 to 9
- prefix_values: bfloat16 [1152, 4, 128], P(('groups', 'seq'), 'tp'), parts along dimension 0, may hold values from -6.5 to 6.5
- prefix_lengths: int32 [16], P('groups'), parts along dimension 0, may hold values from 1 to 72
- decode_queries: bfloat16 [32, 64, 128], P(('groups', 'seq'), 'tp'), parts along dimension 0, may hold values from -180 to 180
- decode_new_keys: bfloat16 [32, 4, 128], P(('groups', 'seq'), 'tp'), parts along dimension 0, may hold values from -6 to 6
- decode_new_values: bfloat16 [32, 4, 128], P(('groups', 'seq'), 'tp'), parts along dimension 0, may hold values from -6 to 6
- decode_key_cache: bfloat16 [64, 256, 4, 128], P(('groups', 'seq'), None, 'tp'), parts along dimension 0, may hold values from -6 to 6
- decode_value_cache: bfloat16 [64, 256, 4, 128], P(('groups', 'seq'), None, 'tp'), parts along dimension 0, may hold values from -6 to 6
- owner_map: int32 [32, 1], P('groups'), parts along dimension 0, may hold values from 0 to 7; in each aligned block of 16 rows (0 to 15, 16 to 31, ...) at most 4 rows name the same one
- decode_lengths: int32 [32], P('groups'), parts along dimension 0, may hold values from 1 to 256
Outputs:
- prefill_out: bfloat16 [128, 64, 128], P(('groups', 'seq'), 'tp'), parts along dimension 0
- decode_out: bfloat16 [64, 64, 128], P(('groups', 'seq'), 'tp'), parts along dimension 0
There are 2 independent parts, one for each index of `groups`. A program takes and returns all parts, laid end to end along the dimension named above; each array names one. Nothing has to cross between parts.
Inputs may be any that keep to these rules, and one draw needn't show every extreme that they name: `owner_map`: no shard owns more than 4 requests, and some shard owns exactly 4.
All inputs are finite; a program needn't handle non-finite values.
Results may differ from a plain program's by a relative error of at most 0.005.
Values may be sent and summed in bfloat16 or wider, within the bound.
No kernel may reach another device: no remote copies, remote signals or barrier semaphores. Data moves between devices by JAX's collectives and lax.ppermute only.
A program may use at most 64 MiB of HBM per device.

v0:
```python
import jax
import jax.numpy as jnp
from jax import lax
from jax.sharding import PartitionSpec as P

LOWEST = -1e30


def lookup_small(table, wanted):
    columns = jnp.arange(table.shape[0], dtype=jnp.int32)
    return jnp.sum(jnp.where(wanted[:, None] == columns[None, :], table[None, :], 0), axis=1)


def block_split(length):
    blocks = 1
    while length // blocks > 512 or length % blocks != 0:
        blocks += 1
    return blocks


def online_step(carried, queries, key_rows, value_rows, allowed):
    running_max, normalizer, weighted = carried
    scale = queries.shape[-1] ** (-0.5)
    scores = (
        jnp.einsum("tkgd,nkd->tkgn", queries, key_rows, preferred_element_type=jnp.float32) * scale
    )
    visible = allowed[:, None, None, :]
    scores = jnp.where(visible, scores, LOWEST)
    new_max = jnp.maximum(running_max, jnp.max(scores, axis=-1))
    weights = jnp.where(visible, jnp.exp(scores - new_max[..., None]), 0.0)
    factor = jnp.exp(running_max - new_max)
    normalizer = normalizer * factor + jnp.sum(weights, axis=-1)
    weighted = weighted * factor[..., None] + jnp.einsum(
        "tkgn,nkd->tkgd",
        weights.astype(jnp.bfloat16),
        value_rows,
        preferred_element_type=jnp.float32,
    )
    return (new_max, normalizer, weighted)


def guarded_step(carried, queries, key_rows, value_rows, allowed):
    return lax.cond(
        jnp.any(allowed),
        lambda inner: online_step(inner, queries, key_rows, value_rows, allowed),
        lambda inner: inner,
        carried,
    )


def fold_rows(carried, queries, key_rows, value_rows, allowed):
    length = key_rows.shape[0]
    blocks = block_split(length)
    if blocks == 1:
        return guarded_step(carried, queries, key_rows, value_rows, allowed)
    width = length // blocks
    stacked = (
        key_rows.reshape((blocks, width) + key_rows.shape[1:]),
        value_rows.reshape((blocks, width) + value_rows.shape[1:]),
        allowed.reshape(allowed.shape[0], blocks, width).transpose(1, 0, 2),
    )

    def visit(inner_carry, parts):
        return (guarded_step(inner_carry, queries, parts[0], parts[1], parts[2]), None)

    carried, unused = lax.scan(visit, carried, stacked)
    return carried


def on_device(
    span_queries,
    span_keys,
    span_values,
    prefix_keys,
    prefix_values,
    prefix_lengths,
    decode_queries,
    decode_new_keys,
    decode_new_values,
    decode_key_cache,
    decode_value_cache,
    owner_map,
    decode_lengths,
):
    device = lax.axis_index("seq")
    tokens_here, heads_here, head_dim = span_queries.shape
    kv_here = span_keys.shape[1]
    group_size = heads_here // kv_here
    queries = span_queries.reshape(tokens_here, kv_here, group_size, head_dim)
    token_index = device * tokens_here + jnp.arange(tokens_here, dtype=jnp.int32)
    prefix_here = prefix_keys.shape[0]
    initial = (
        jnp.full((tokens_here, kv_here, group_size), LOWEST, jnp.float32),
        jnp.zeros((tokens_here, kv_here, group_size), jnp.float32),
        jnp.zeros((tokens_here, kv_here, group_size, head_dim), jnp.float32),
    )
    stride = prefix_here + tokens_here
    both_keys = jnp.concatenate([prefix_keys, span_keys], axis=0)
    both_values = jnp.concatenate([prefix_values, span_values], axis=0)
    carried = initial
    key_rows = lax.all_gather(both_keys, "seq", axis=0, tiled=True)
    value_rows = lax.all_gather(both_values, "seq", axis=0, tiled=True)
    length = key_rows.shape[0]
    shards = length // stride
    tail = key_rows.shape[1:]
    keys_split = key_rows.reshape((shards, stride) + tail)
    values_split = value_rows.reshape((shards, stride) + tail)
    prefix_k = keys_split[:, :prefix_here].reshape((shards * prefix_here,) + tail)
    prefix_v = values_split[:, :prefix_here].reshape((shards * prefix_here,) + tail)
    span_k = keys_split[:, prefix_here:].reshape((shards * tokens_here,) + tail)
    span_v = values_split[:, prefix_here:].reshape((shards * tokens_here,) + tail)
    prefix_position = jnp.arange(shards * prefix_here, dtype=jnp.int32)
    prefix_ok = prefix_position % prefix_here < lookup_small(
        prefix_lengths, prefix_position // prefix_here
    )
    carried = fold_rows(
        carried,
        queries,
        prefix_k,
        prefix_v,
        jnp.broadcast_to(prefix_ok[None, :], (tokens_here, prefix_k.shape[0])),
    )
    span_position = jnp.arange(shards * tokens_here, dtype=jnp.int32)
    carried = fold_rows(
        carried, queries, span_k, span_v, span_position[None, :] <= token_index[:, None]
    )
    running_max, normalizer, weighted = carried
    prefill_out = (
        (weighted / normalizer[..., None])
        .reshape(tokens_here, heads_here, head_dim)
        .astype(jnp.bfloat16)
    )
    owners = owner_map[:, 0]
    requests = owners.shape[0]
    order = jnp.arange(requests, dtype=jnp.int32)
    earlier = (owners[None, :] == owners[:, None]) & (order[None, :] < order[:, None])
    ranking = jnp.sum(earlier.astype(jnp.int32), axis=1)
    slots_here = decode_key_cache.shape[0]
    slot_ids = jnp.arange(slots_here, dtype=jnp.int32)
    query_rows = lax.all_gather(decode_queries, "seq", axis=0, tiled=True)
    new_keys = lax.all_gather(decode_new_keys, "seq", axis=0, tiled=True)
    new_values = lax.all_gather(decode_new_values, "seq", axis=0, tiled=True)
    chosen = (owners == device)[None, :] & (ranking[None, :] == slot_ids[:, None])
    selector = chosen.astype(jnp.bfloat16)
    picked_queries = jnp.einsum(
        "sn,nhd->shd", selector, query_rows, preferred_element_type=jnp.float32
    )
    picked_keys = jnp.einsum("sn,nkd->skd", selector, new_keys, preferred_element_type=jnp.float32)
    picked_values = jnp.einsum(
        "sn,nkd->skd", selector, new_values, preferred_element_type=jnp.float32
    )
    picked_lengths = jnp.sum(jnp.where(chosen, decode_lengths[None, :], 0), axis=1)
    context = decode_key_cache.shape[1]
    grouped = picked_queries.astype(jnp.bfloat16).reshape(slots_here, kv_here, group_size, head_dim)
    own_keys = picked_keys.astype(jnp.bfloat16)
    own_values = picked_values.astype(jnp.bfloat16)
    scale = head_dim ** (-0.5)
    scores = (
        jnp.einsum("skgd,sckd->skgc", grouped, decode_key_cache, preferred_element_type=jnp.float32)
        * scale
    )
    visible = (jnp.arange(context, dtype=jnp.int32)[None, :] < picked_lengths[:, None])[
        :, None, None, :
    ]
    scores = jnp.where(visible, scores, LOWEST)
    own_score = (
        jnp.einsum("skgd,skd->skg", grouped, own_keys, preferred_element_type=jnp.float32) * scale
    )
    top_score = jnp.maximum(jnp.max(scores, axis=-1), own_score)
    weights = jnp.where(visible, jnp.exp(scores - top_score[..., None]), 0.0)
    own_weight = jnp.exp(own_score - top_score)
    total_weight = jnp.sum(weights, axis=-1) + own_weight
    rounded_own = lax.optimization_barrier(own_weight.astype(jnp.bfloat16)).astype(jnp.float32)
    mixed = jnp.einsum(
        "skgc,sckd->skgd",
        weights.astype(jnp.bfloat16),
        decode_value_cache,
        preferred_element_type=jnp.float32,
    )
    mixed = mixed + rounded_own[..., None] * own_values.astype(jnp.float32)[:, :, None, :]
    count_here = jnp.sum((owners == device).astype(jnp.int32))
    used = (slot_ids < count_here)[:, None, None, None]
    decode_out = (
        jnp.where(used, mixed / total_weight[..., None], 0.0)
        .reshape(slots_here, heads_here, head_dim)
        .astype(jnp.bfloat16)
    )
    return (prefill_out, decode_out)


def solution(mesh):
    return jax.shard_map(
        on_device,
        mesh=mesh,
        in_specs=(
            P(("groups", "seq"), "tp", None),
            P(("groups", "seq"), "tp", None),
            P(("groups", "seq"), "tp", None),
            P(("groups", "seq"), "tp", None),
            P(("groups", "seq"), "tp", None),
            P("groups"),
            P(("groups", "seq"), "tp", None),
            P(("groups", "seq"), "tp", None),
            P(("groups", "seq"), "tp", None),
            P(("groups", "seq"), None, "tp", None),
            P(("groups", "seq"), None, "tp", None),
            P("groups", None),
            P("groups"),
        ),
        out_specs=(P(("groups", "seq"), "tp", None), P(("groups", "seq"), "tp", None)),
        check_vma=False,
    )
```

profile of v0, /device:TPU:0, one launch (start us, length us, event | category | flops | bytes accessed | tf_op | source)
XLA Modules:
  0.0 148.8 jit_solution(11207647977653412298)
XLA Ops:
  0.6 0.0 copy-start
  0.6 0.0 copy-start.2
  0.7 0.7 iota_compare_fusion.3
  2.0 0.7 select_reduce_fusion
  2.8 0.1 reduce_sum.68
  2.9 0.0 copy-start.5
  2.9 0.0 copy-done.2
  2.9 0.7 copy-done.5
  3.6 0.1 pad_maximum_fusion
  3.6 32.7 %all_gather.15 = bf16[640,2,128]{2,1,0:T(2,128)(2,1)S(1)} all-gather(bf16[80,2,128]{2,1,0:T(2,128)(2,1)S(1)} %pad_maximum_fusion), channel_id=1, replica_groups=mesh['groups'=2,'seq'=8,'tp'=2] {'seq'}, dimensions={0}, use_global_device_ids=true | all-gather | bytes 368640 | tf_op jit(solution)/shard_map/all_gather | solution.py:101
  36.4 0.0 copy-start.1
  36.4 0.8 copy-done.1
  37.2 0.0 copy-start.3
  37.2 0.0 copy-start.6
  37.2 0.8 copy-done.3
  38.0 0.0 copy-done.6
  38.0 0.1 pad_maximum_fusion.1
  38.1 30.9 %all_gather.16 = bf16[640,2,128]{2,1,0:T(2,128)(2,1)S(1)} all-gather(bf16[80,2,128]{2,1,0:T(2,128)(2,1)S(1)} %pad_maximum_fusion.1), channel_id=1, replica_groups=mesh['groups'=2,'seq'=8,'tp'=2] {'seq'}, dimensions={0}, use_global_device_ids=true | all-gather | bytes 368640 | tf_op jit(solution)/shard_map/all_gather | solution.py:102
  69.1 4.4 %while.14 = (s32[]{:T(128)}, f32[8,2,16]{2,0,1:T(8,128)S(1)}, f32[8,2,16]{2,0,1:T(8,128)S(1)}, f32[8,2,16,128]{3,2,0,1:T(8,128)S(1)}, pred[2,8,288]{2,1,0:T(8,12...) while((s32[]{:T(128)}, f32[8,2,16]{2,0,1:T(8,128)S(1)}, ...), condition=%wide.region_8.9_spmd, body=%wide.region_2.8_spmd.sunk | while | flops 38480640 | bytes 1649647 | solution.py:66
  69.2 0.7 fusion.72
  70.5 0.9 conditional.4
  70.5 0.3 fusion.67
  70.8 0.2 fusion.4
  71.1 0.3 fusion.2
  71.4 0.7 fusion.72
  72.7 0.9 conditional.4
  72.7 0.3 fusion.67
  73.0 0.2 fusion.4
  73.3 0.3 fusion.2
  73.6 0.7 conditional.2
  73.6 0.3 fusion.68
  73.9 0.2 fusion.20
  74.1 0.2 fusion.16
  74.3 0.1 divide_convert_fusion
  74.5 0.0 copy-start.4
  74.5 0.6 copy.71
  75.1 0.1 copy-done.4
  75.2 30.5 %all_gather.17 = bf16[16,32,128]{2,1,0:T(8,128)(2,1)S(1)} all-gather(bf16[2,32,128]{2,1,0:T(8,128)(2,1)S(1)} %copy-done.4), channel_id=1, replica_groups=mesh['groups'=2,'seq'=8,'tp'=2] {'seq'}, dimensions={0}, use_global_device_ids=true | all-gather | bytes 147456 | tf_op jit(solution)/shard_map/all_gather | solution.py:140
  105.7 0.0 copy-start.10
  105.7 0.7 copy-done.10
  106.3 0.2 convert_reduce_fusion
  106.5 0.6 convert_reduce_fusion.1
  107.2 0.0 copy-start.9
  107.2 0.7 copy-done.9
  107.8 0.1 select_reduce_fusion.1
  107.9 0.2 convolution_convert_fusion
  108.1 0.0 copy-start.11
  108.1 0.1 iota_compare_fusion.2
  108.2 0.0 copy-done
  108.2 0.3 fusion.69
  108.5 0.0 copy-start.7
  108.5 0.7 copy-done.7
  109.2 20.5 %all_gather.18 = bf16[16,2,128]{2,1,0:T(2,128)(2,1)S(1)} all-gather(bf16[2,2,128]{2,1,0:T(2,128)(2,1)S(1)} %copy-done.7), channel_id=1, replica_groups=mesh['groups'=2,'seq'=8,'tp'=2] {'seq'}, dimensions={0}, use_global_device_ids=true | all-gather | bytes 9216 | tf_op jit(solution)/shard_map/all_gather | solution.py:141
  129.7 0.1 fusion.36
  129.8 0.1 fusion.46
  129.9 0.2 fusion.40
  130.1 0.0 copy-start.8
  130.2 0.7 copy-done.8
  130.8 16.3 %all_gather.19 = bf16[16,2,128]{2,1,0:T(2,128)(2,1)S(1)} all-gather(bf16[2,2,128]{2,1,0:T(2,128)(2,1)S(1)} %copy-done.8), channel_id=1, replica_groups=mesh['groups'=2,'seq'=8,'tp'=2] {'seq'}, dimensions={0}, use_global_device_ids=true | all-gather | bytes 9216 | tf_op jit(solution)/shard_map/all_gather | solution.py:142
  147.1 0.1 fusion.35
  147.2 0.6 iota_compare_fusion.5
  147.9 0.0 copy-done.11
  147.9 0.9 fusion.34
  (26 shorter events, 0.3 us)
Async XLA Ops:
  0.6 107.6 %copy-start = (bf16[4,256,2,128]{3,2,1,0:T(2,128)(2,1)S(1)}, bf16[4,256,2,128]{3,2,1,0:T(2,128)(2,1)}, u32[]{:S(2)}) copy-start(bf16[4,256,2,128]{3,2,1,0:T(2,128)(2,1)} %param.28) | copy-start | bytes 1572868
  0.6 2.3 %copy-start.2 = (bf16[72,2,128]{2,1,0:T(2,128)(2,1)S(1)}, bf16[72,2,128]{2,1,0:T(2,128)(2,1)}, u32[]{:S(2)}) copy-start(bf16[72,2,128]{2,1,0:T(2,128)(2,1)} %param.22) | copy-start | bytes 110596
  2.9 0.7 copy-start.5
  36.4 0.8 copy-start.1
  37.2 0.8 copy-start.3
  37.2 0.8 copy-start.6
  74.5 0.7 copy-start.4
  105.7 0.7 copy-start.10
  107.2 0.7 copy-start.9
  108.1 39.8 %copy-start.11 = (bf16[4,256,2,128]{3,2,1,0:T(2,128)(2,1)S(1)}, bf16[4,256,2,128]{3,2,1,0:T(2,128)(2,1)}, u32[]{:S(2)}) copy-start(bf16[4,256,2,128]{3,2,1,0:T(2,128)(2,1)} %param.29) | copy-start | bytes 1572868
  108.5 0.7 copy-start.7
  130.1 0.7 copy-start.8
where the time goes:
time: 149 us
  blocking collectives  131 us (88%)
  local copies, waits for them, and re-layouts  5.93 us (4%)
  other arithmetic  5.57 us (4%)
  matrix products  3.39 us (2%)
  between operations  1.53 us (1%)
  loops' own time  1.5 us (1%)
    all_gather x1, blocking collectives, on_device(): key_rows = lax.all_gather(both_keys, 'seq', axis=0, tiled=True)  32.7 us
    all_gather x1, blocking collectives, on_device(): value_rows = lax.all_gather(both_values, 'seq', axis=0, tiled=True)  30.9 us
    all_gather x1, blocking collectives, on_device(): query_rows = lax.all_gather(decode_queries, 'seq', axis=0, tiled=True)  30.5 us
    all_gather x1, blocking collectives, on_device(): new_keys = lax.all_gather(decode_new_keys, 'seq', axis=0, tiled=True)  20.5 us
    all_gather x1, blocking collectives, on_device(): new_values = lax.all_gather(decode_new_values, 'seq', axis=0, tiled=True)  16.3 us
    unnamed x24, local copies, waits for them, and re-layouts  4.99 us

commit v1 on v0

--- a/solution.py
+++ b/solution.py
@@ -4,6 +4,18 @@
 from jax.sharding import PartitionSpec as P
 
 LOWEST = -1e30
+
+
+def ring_product(x, axis, dim, term):
+    length, index, rows = (lax.axis_size(axis), lax.axis_index(axis), x.shape[dim])
+    right = [(i, (i + 1) % length) for i in range(length)]
+    block, total = (x, None)
+    for hop in range(length):
+        following = lax.ppermute(block, axis, right) if hop < length - 1 else None
+        update = term(block, (index - hop) % length * rows)
+        total = update if total is None else total + update
+        block = following
+    return total
 
 
 def lookup_small(table, wanted):
@@ -137,13 +149,20 @@
     ranking = jnp.sum(earlier.astype(jnp.int32), axis=1)
     slots_here = decode_key_cache.shape[0]
     slot_ids = jnp.arange(slots_here, dtype=jnp.int32)
-    query_rows = lax.all_gather(decode_queries, "seq", axis=0, tiled=True)
     new_keys = lax.all_gather(decode_new_keys, "seq", axis=0, tiled=True)
     new_values = lax.all_gather(decode_new_values, "seq", axis=0, tiled=True)
     chosen = (owners == device)[None, :] & (ranking[None, :] == slot_ids[:, None])
     selector = chosen.astype(jnp.bfloat16)
-    picked_queries = jnp.einsum(
-        "sn,nhd->shd", selector, query_rows, preferred_element_type=jnp.float32
+    picked_queries = ring_product(
+        decode_queries,
+        "seq",
+        0,
+        lambda part, offset: jnp.einsum(
+            "sn,nhd->shd",
+            lax.dynamic_slice_in_dim(selector, offset, part.shape[0], axis=1),
+            part,
+            preferred_element_type=jnp.float32,
+        ),
     )
     picked_keys = jnp.einsum("sn,nkd->skd", selector, new_keys, preferred_element_type=jnp.float32)
     picked_values = jnp.einsum(

time: 149 us -> 158 us (1.060)
  waiting for transfers between devices: 0 us -> 35.3 us
  blocking collectives: 131 us -> 97.3 us
  starting transfers between devices: 0 us -> 5.05 us
  matrix products: 3.39 us -> 5.25 us
    ppermute x0 -> x7, waiting for transfers between devices: none -> 35.3 us  [ring_product(): following = lax.ppermute(block, axis, right) if hop < length - 1 else None]
    all_gather x1 -> x0, blocking collectives: 30.5 us -> none  [on_device(): query_rows = lax.all_gather(decode_queries, 'seq', axis=0, tiled=True)]
    ppermute x0 -> x7, starting transfers between devices: none -> 5.05 us  [ring_product(): following = lax.ppermute(block, axis, right) if hop < length - 1 else None]
    unnamed x24 -> x27, local copies, waits for them, and re-layouts: 4.99 us -> 5.23 us
  transfers between devices with their start and end apart: 0 -> 7, of which waited for: 0 -> 6; matrix products, arithmetic and copies ran while one was open for 0% -> 6% of each run, Pallas kernels for 0% -> 0%
where the time goes in v1:
time: 158 us; the launch traced here: 157 us
  blocking collectives  97.3 us (62%)
  waiting for transfers between devices  35.3 us (22%)
  local copies, waits for them, and re-layouts  6.16 us (4%)
  matrix products  5.25 us (3%)
  starting transfers between devices  5.05 us (3%)
  other arithmetic  4.9 us (3%)
  between operations  1.71 us (1%)
    ppermute x7, waiting for transfers between devices, ring_product(): following = lax.ppermute(block, axis, right) if hop < length - 1 else None  35.3 us
    all_gather x1, blocking collectives, on_device(): key_rows = lax.all_gather(both_keys, 'seq', axis=0, tiled=True)  31.2 us
    all_gather x1, blocking collectives, on_device(): value_rows = lax.all_gather(both_values, 'seq', axis=0, tiled=True)  30.9 us
    all_gather x1, blocking collectives, on_device(): new_keys = lax.all_gather(decode_new_keys, 'seq', axis=0, tiled=True)  19 us
    all_gather x1, blocking collectives, on_device(): new_values = lax.all_gather(decode_new_values, 'seq', axis=0, tiled=True)  16.3 us
    unnamed x27, local copies, waits for them, and re-layouts  5.23 us
    ppermute x7, starting transfers between devices, ring_product(): following = lax.ppermute(block, axis, right) if hop < length - 1 else None  5.05 us
  transfers between devices with their start and end apart: 7, of which 6 were waited for; matrix products, arithmetic and copies ran while one was open for 6% of the time, Pallas kernels for 0%

profile of v1, /device:TPU:0, one launch (start us, length us, event | category | flops | bytes accessed | tf_op | source)
XLA Modules:
  0.0 157.0 jit_solution(15006418897313105475)
XLA Ops:
  0.6 0.0 copy-start
  0.6 0.8 copy.82
  1.4 3.0 %collective-permute-start = (bf16[2,32,128]{2,0,1:T(2,128)(2,1)S(1)}, bf16[2,32,128]{2,0,1:T(2,128)(2,1)S(1)}, u32[]{:S(2)}, u32[]{:S(2)}) collective-permute-start(bf16[2,32,128]{2,0,1:T(2,128)(2,1)S(1)} %copy.82), channel_id=1, source_target_pairs={{0,2},{2,4},{4,6},{6,8},{8,10},{10,12},{12,14},{14,0},{1,3},{3,5},... | collective-permute-start | bytes 49160 | tf_op jit(solution)/shard_map/ppermute | solution.py:14
  4.5 0.7 iota_compare_fusion.4
  5.9 0.1 select_reduce_fusion
  5.9 0.1 reduce_sum.68
  6.1 0.7 copy-done.5
  6.7 0.1 pad_maximum_fusion
  6.8 31.2 %all_gather.12 = bf16[640,2,128]{2,1,0:T(2,128)(2,1)S(1)} all-gather(bf16[80,2,128]{2,1,0:T(2,128)(2,1)S(1)} %pad_maximum_fusion), channel_id=1, replica_groups=mesh['groups'=2,'seq'=8,'tp'=2] {'seq'}, dimensions={0}, use_global_device_ids=true | all-gather | bytes 368640 | tf_op jit(solution)/shard_map/all_gather | solution.py:113
  38.1 0.8 copy-done.1
  38.9 0.8 copy-done.4
  39.7 0.1 pad_maximum_fusion.1
  39.7 30.9 %all_gather.13 = bf16[640,2,128]{2,1,0:T(2,128)(2,1)S(1)} all-gather(bf16[80,2,128]{2,1,0:T(2,128)(2,1)S(1)} %pad_maximum_fusion.1), channel_id=1, replica_groups=mesh['groups'=2,'seq'=8,'tp'=2] {'seq'}, dimensions={0}, use_global_device_ids=true | all-gather | bytes 368640 | tf_op jit(solution)/shard_map/all_gather | solution.py:114
  70.7 0.0 copy-start.10
  70.8 4.2 %while.14 = (s32[]{:T(128)}, f32[8,2,16]{2,0,1:T(8,128)S(1)}, f32[8,2,16]{2,0,1:T(8,128)S(1)}, f32[8,2,16,128]{3,2,0,1:T(8,128)S(1)}, pred[2,8,288]{2,1,0:T(8,12...) while((s32[]{:T(128)}, f32[8,2,16]{2,0,1:T(8,128)S(1)}, ...), condition=%wide.region_8.9_spmd, body=%wide.region_2.8_spmd.sunk | while | flops 38480640 | bytes 1649647 | solution.py:78
  70.8 0.6 fusion.97
  72.0 0.9 conditional.4
  72.0 0.3 fusion.85
  72.3 0.2 fusion.4
  72.5 0.3 fusion.2
  72.9 0.6 fusion.97
  74.1 0.9 conditional.4
  74.1 0.3 fusion.85
  74.4 0.2 fusion.4
  74.7 0.3 fusion.2
  75.0 0.6 convert_reduce_fusion.1
  75.6 0.2 convert_reduce_fusion
  75.8 0.1 fusion.52
  75.9 0.6 copy-done.11
  76.5 0.1 select_reduce_fusion.1
  76.6 0.1 iota_compare_fusion.3
  76.6 0.6 copy-done.7
  77.2 19.0 %all_gather.14 = bf16[16,2,128]{2,1,0:T(2,128)(2,1)S(1)} all-gather(bf16[2,2,128]{2,1,0:T(2,128)(2,1)S(1)} %copy-done.7), channel_id=1, replica_groups=mesh['groups'=2,'seq'=8,'tp'=2] {'seq'}, dimensions={0}, use_global_device_ids=true | all-gather | bytes 9216 | tf_op jit(solution)/shard_map/all_gather | solution.py:152
  96.3 0.3 fusion.37
  96.5 0.4 copy-done.8
  96.9 16.3 %all_gather.15 = bf16[16,2,128]{2,1,0:T(2,128)(2,1)S(1)} all-gather(bf16[2,2,128]{2,1,0:T(2,128)(2,1)S(1)} %copy-done.8), channel_id=1, replica_groups=mesh['groups'=2,'seq'=8,'tp'=2] {'seq'}, dimensions={0}, use_global_device_ids=true | all-gather | bytes 9216 | tf_op jit(solution)/shard_map/all_gather | solution.py:153
  113.2 0.3 fusion.36
  113.5 0.7 conditional.2
  113.5 0.3 fusion.86
  113.7 0.2 fusion.20
  114.0 0.2 fusion.16
  114.2 0.1 divide_convert_fusion
  114.3 0.6 copy-done.2
  114.9 0.2 fusion.63
  115.1 0.7 iota_compare_fusion.5
  115.9 0.6 copy.81
  116.6 2.0 %collective-permute-start.1 = (bf16[2,32,128]{2,0,1:T(2,128)(2,1)S(1)}, bf16[2,32,128]{2,0,1:T(2,128)(2,1)S(1)}, u32[]{:S(2)}, u32[]{:S(2)}) collective-permute-start(bf16[2,32,128]{2,0,1:T(2,128)(2,1)S(1)} %collective-permute-done), channel_id=1, source_target_pairs={{0,2},{2,4},{4,6},{6,8},{8,10},{10,12},{12,14},{14,0},{1,3},{3,5},... | collective-permute-start | bytes 49160 | tf_op jit(solution)/shard_map/ppermute | solution.py:14
  118.6 0.2 convolution_add_fusion.6
  118.8 4.2 %collective-permute-done.1 = bf16[2,32,128]{2,0,1:T(2,128)(2,1)S(1)} collective-permute-done((bf16[2,32,128]{2,0,1:T(2,128)(2,1)S(1)}, bf16[2,32,128]{2,0,1:T(2,128)(2,1)S(1)}, u32[]{:S(2)}, u32[]{:S(2)}) %collective-permute-start.1) | collective-permute-done | bytes 16416 | tf_op jit(solution)/shard_map/ppermute | solution.py:14
  123.0 0.2 convolution_add_fusion.5
  123.2 6.2 %collective-permute-done.2 = bf16[2,32,128]{2,0,1:T(2,128)(2,1)S(1)} collective-permute-done((bf16[2,32,128]{2,0,1:T(2,128)(2,1)S(1)}, bf16[2,32,128]{2,0,1:T(2,128)(2,1)S(1)}, u32[]{:S(2)}, u32[]{:S(2)}) %collective-permute-start.2) | collective-permute-done | bytes 16416 | tf_op jit(solution)/shard_map/ppermute | solution.py:14
  129.5 0.2 convolution_add_fusion.4
  129.7 6.2 %collective-permute-done.3 = bf16[2,32,128]{2,0,1:T(2,128)(2,1)S(1)} collective-permute-done((bf16[2,32,128]{2,0,1:T(2,128)(2,1)S(1)}, bf16[2,32,128]{2,0,1:T(2,128)(2,1)S(1)}, u32[]{:S(2)}, u32[]{:S(2)}) %collective-permute-start.3) | collective-permute-done | bytes 16416 | tf_op jit(solution)/shard_map/ppermute | solution.py:14
  135.9 0.2 convolution_add_fusion.3
  136.1 6.2 %collective-permute-done.4 = bf16[2,32,128]{2,0,1:T(2,128)(2,1)S(1)} collective-permute-done((bf16[2,32,128]{2,0,1:T(2,128)(2,1)S(1)}, bf16[2,32,128]{2,0,1:T(2,128)(2,1)S(1)}, u32[]{:S(2)}, u32[]{:S(2)}) %collective-permute-start.4) | collective-permute-done | bytes 16416 | tf_op jit(solution)/shard_map/ppermute | solution.py:14
  142.3 0.2 convolution_add_fusion.2
  142.6 6.2 %collective-permute-done.5 = bf16[2,32,128]{2,0,1:T(2,128)(2,1)S(1)} collective-permute-done((bf16[2,32,128]{2,0,1:T(2,128)(2,1)S(1)}, bf16[2,32,128]{2,0,1:T(2,128)(2,1)S(1)}, u32[]{:S(2)}, u32[]{:S(2)}) %collective-permute-start.5) | collective-permute-done | bytes 16416 | tf_op jit(solution)/shard_map/ppermute | solution.py:14
  148.8 0.2 convolution_add_fusion.1
  149.0 6.2 %collective-permute-done.6 = bf16[2,32,128]{2,0,1:T(2,128)(2,1)S(1)} collective-permute-done((bf16[2,32,128]{2,0,1:T(2,128)(2,1)S(1)}, bf16[2,32,128]{2,0,1:T(2,128)(2,1)S(1)}, u32[]{:S(2)}, u32[]{:S(2)}) %collective-permute-start.6) | collective-permute-done | bytes 16416 | tf_op jit(solution)/shard_map/ppermute | solution.py:14
  155.2 0.2 fusion.35
  155.4 0.1 fusion.46
  155.6 0.3 fusion.87
  155.9 0.2 fusion.40
  156.1 0.9 fusion.34
  (49 shorter events, 0.4 us)
Async XLA Ops:
  0.6 154.9 %copy-start = (bf16[4,256,2,128]{3,2,1,0:T(2,128)(2,1)S(1)}, bf16[4,256,2,128]{3,2,1,0:T(2,128)(2,1)}, u32[]{:S(2)}) copy-start(bf16[4,256,2,128]{3,2,1,0:T(2,128)(2,1)} %param.28) | copy-start | bytes 1572868
  1.4 4.6 %copy-start.3 = (bf16[72,2,128]{2,1,0:T(2,128)(2,1)S(1)}, bf16[72,2,128]{2,1,0:T(2,128)(2,1)}, u32[]{:S(2)}) copy-start(bf16[72,2,128]{2,1,0:T(2,128)(2,1)} %param.22) | copy-start | bytes 110596
  1.4 115.1 %collective-permute-start = (bf16[2,32,128]{2,0,1:T(2,128)(2,1)S(1)}, bf16[2,32,128]{2,0,1:T(2,128)(2,1)S(1)}, u32[]{:S(2)}, u32[]{:S(2)}) collective-permute-start(bf16[2,32,128]{2,0,1:T(2,128)(2,1)S(1)} %copy.82), channel_id=1, source_target_pairs={{0,2},{2,4},{4,6},{6,8},{8,10},{10,12},{12,14},{14,0},{1,3},{3,5},... | collective-permute-start | bytes 49160 | tf_op jit(solution)/shard_map/ppermute | solution.py:14
  5.2 0.7 copy-start.9
  6.0 0.7 copy-start.5
  38.0 0.8 copy-start.1
  38.9 0.8 copy-start.4
  38.9 0.8 copy-start.6
  70.7 4.2 %copy-start.10 = (s32[16,1]{0,1:T(1,128)S(1)}, s32[16,1]{0,1:T(1,128)}, u32[]{:S(2)}) copy-start(s32[16,1]{0,1:T(1,128)} %param.30) | copy-start | bytes 196
  75.8 0.7 copy-start.11
  76.6 0.7 copy-start.7
  96.3 0.7 copy-start.8
  114.2 0.7 copy-start.2
  116.6 6.4 %collective-permute-start.1 = (bf16[2,32,128]{2,0,1:T(2,128)(2,1)S(1)}, bf16[2,32,128]{2,0,1:T(2,128)(2,1)S(1)}, u32[]{:S(2)}, u32[]{:S(2)}) collective-permute-start(bf16[2,32,128]{2,0,1:T(2,128)(2,1)S(1)} %collective-permute-done), channel_id=1, source_target_pairs={{0,2},{2,4},{4,6},{6,8},{8,10},{10,12},{12,14},{14,0},{1,3},{3,5},... | collective-permute-start | bytes 49160 | tf_op jit(solution)/shard_map/ppermute | solution.py:14
  123.0 6.4 %collective-permute-start.2 = (bf16[2,32,128]{2,0,1:T(2,128)(2,1)S(1)}, bf16[2,32,128]{2,0,1:T(2,128)(2,1)S(1)}, u32[]{:S(2)}, u32[]{:S(2)}) collective-permute-start(bf16[2,32,128]{2,0,1:T(2,128)(2,1)S(1)} %collective-permute-done.1), channel_id=1, source_target_pairs={{0,2},{2,4},{4,6},{6,8},{8,10},{10,12},{12,14},{14,0},{1,3},{3,5},... | collective-permute-start | bytes 49160 | tf_op jit(solution)/shard_map/ppermute | solution.py:14
  129.5 6.4 %collective-permute-start.3 = (bf16[2,32,128]{2,0,1:T(2,128)(2,1)S(1)}, bf16[2,32,128]{2,0,1:T(2,128)(2,1)S(1)}, u32[]{:S(2)}, u32[]{:S(2)}) collective-permute-start(bf16[2,32,128]{2,0,1:T(2,128)(2,1)S(1)} %collective-permute-done.2), channel_id=1, source_target_pairs={{0,2},{2,4},{4,6},{6,8},{8,10},{10,12},{12,14},{14,0},{1,3},{3,5},... | collective-permute-start | bytes 49160 | tf_op jit(solution)/shard_map/ppermute | solution.py:14
  135.9 6.4 %collective-permute-start.4 = (bf16[2,32,128]{2,0,1:T(2,128)(2,1)S(1)}, bf16[2,32,128]{2,0,1:T(2,128)(2,1)S(1)}, u32[]{:S(2)}, u32[]{:S(2)}) collective-permute-start(bf16[2,32,128]{2,0,1:T(2,128)(2,1)S(1)} %collective-permute-done.3), channel_id=1, source_target_pairs={{0,2},{2,4},{4,6},{6,8},{8,10},{10,12},{12,14},{14,0},{1,3},{3,5},... | collective-permute-start | bytes 49160 | tf_op jit(solution)/shard_map/ppermute | solution.py:14
  142.3 6.4 %collective-permute-start.5 = (bf16[2,32,128]{2,0,1:T(2,128)(2,1)S(1)}, bf16[2,32,128]{2,0,1:T(2,128)(2,1)S(1)}, u32[]{:S(2)}, u32[]{:S(2)}) collective-permute-start(bf16[2,32,128]{2,0,1:T(2,128)(2,1)S(1)} %collective-permute-done.4), channel_id=1, source_target_pairs={{0,2},{2,4},{4,6},{6,8},{8,10},{10,12},{12,14},{14,0},{1,3},{3,5},... | collective-permute-start | bytes 49160 | tf_op jit(solution)/shard_map/ppermute | solution.py:14
  148.8 6.4 %collective-permute-start.6 = (bf16[2,32,128]{2,0,1:T(2,128)(2,1)S(1)}, bf16[2,32,128]{2,0,1:T(2,128)(2,1)S(1)}, u32[]{:S(2)}, u32[]{:S(2)}) collective-permute-start(bf16[2,32,128]{2,0,1:T(2,128)(2,1)S(1)} %collective-permute-done.5), channel_id=1, source_target_pairs={{0,2},{2,4},{4,6},{6,8},{8,10},{10,12},{12,14},{14,0},{1,3},{3,5},... | collective-permute-start | bytes 49160 | tf_op jit(solution)/shard_map/ppermute | solution.py:14
  149.0 7.2 %copy-start.12 = (bf16[4,256,2,128]{3,2,1,0:T(2,128)(2,1)S(1)}, bf16[4,256,2,128]{3,2,1,0:T(2,128)(2,1)}, u32[]{:S(2)}) copy-start(bf16[4,256,2,128]{3,2,1,0:T(2,128)(2,1)} %param.29) | copy-start | bytes 1572868
